TPU v7x, 8 devices: a whole 2x2x1 slice. The times are simulated.
8 devices in a mesh: dp: 1 (over z), sp: 8 (over x, y, core).
Axes of the slice: x: 2, y: 2, z: 1, core: 2. Of those that a mesh axis runs over, the one named last changes fastest.
Arguments:
- q: bfloat16 [32, 8, 256], P('dp')
- k: bfloat16 [32, 4096, 8, 256], P('dp', 'sp')
- v: bfloat16 [32, 4096, 8, 256], P('dp', 'sp')
Outputs:
- q: bfloat16 [32, 8, 256], P('dp')
All inputs are finite; a program needn't handle non-finite values.
Results may differ from a plain program's by a relative error of at most 0.012.
Values are sent between devices in bfloat16 or wider.
A program may use at most 2 GiB of HBM per device.

v0:
```python
import functools
import math

import jax
import jax.numpy as jnp
from jax import lax
from jax.experimental import pallas as pl
from jax.experimental.pallas import tpu as pltpu
from jax.sharding import PartitionSpec as P

SLOTS = 3
TILE = 256
LANES = 128


def peers_of(me):
    x, y, core = me // 4, (me // 2) % 2, me % 2
    for dx, dy, dc in ((1, 1, 1), (1, 1, 0), (1, 0, 1), (1, 0, 0), (0, 1, 1), (0, 1, 0), (0, 0, 1)):
        px = 1 - x if dx else x
        py = 1 - y if dy else y
        pc = 1 - core if dc else core
        yield px * 4 + py * 2 + pc


def kernel(n, q_hbm, k_hbm, v_hbm, o_ref, q_buf, k_buf, v_buf, p_buf, parts, stats, q_sem, k_sem, v_sem, send_sem, recv_sem):
    seqs, rows, head = k_hbm.shape
    heads = q_hbm.shape[1]
    tiles = rows // TILE
    log2e_scaled = math.log2(math.e) * head**-0.5
    me = lax.axis_index("sp")
    peers = list(peers_of(me))

    def k_copy(b):
        slot = lax.rem(b, SLOTS)
        return pltpu.make_async_copy(k_hbm.at[b], k_buf.at[slot], k_sem.at[slot])

    def v_copy(b):
        slot = lax.rem(b, SLOTS)
        return pltpu.make_async_copy(v_hbm.at[b], v_buf.at[slot], v_sem.at[slot])

    def to(peer, ref, send, recv):
        return pltpu.make_async_remote_copy(
            src_ref=ref, dst_ref=ref, send_sem=send, recv_sem=recv, device_id={"sp": peer}, device_id_type=pl.DeviceIdType.MESH
        )

    pltpu.make_async_copy(q_hbm, q_buf, q_sem).start()
    k_copy(0).start()
    for b in range(1, SLOTS):
        k_copy(b).start()
        v_copy(b - 1).start()
    v_copy(SLOTS - 1).start()

    barrier = pltpu.get_barrier_semaphore()
    for peer in peers:
        pl.semaphore_signal(barrier, inc=1, device_id={"sp": peer}, device_id_type=pl.DeviceIdType.MESH)

    own = lax.broadcasted_iota(jnp.int32, (heads, TILE), 1) % heads == lax.broadcasted_iota(jnp.int32, (heads, TILE), 0)
    lane = lax.broadcasted_iota(jnp.int32, (heads, LANES), 1)

    def weigh(b, stat):
        slot = lax.rem(b, SLOTS)
        q = q_buf[b]
        scores = []
        for t in range(tiles):
            s = lax.dot_general(q, k_buf[slot, t * TILE : (t + 1) * TILE, :], (((1,), (1,)), ((), ())), preferred_element_type=jnp.float32)
            scores.append(jnp.where(own, s, -jnp.inf))
        high = jnp.max(functools.reduce(jnp.maximum, scores), -1, keepdims=True)
        total = None
        for t in range(tiles):
            w = jnp.exp2((scores[t] - high) * log2e_scaled)
            p_buf[:, t * TILE : (t + 1) * TILE] = w.astype(jnp.bfloat16)
            total = w if total is None else total + w
        total = jnp.sum(total, -1, keepdims=True)
        return jnp.where(lane == b, high, jnp.where(lane == b + LANES // 2, total, stat))

    def gather_values(b):
        slot = lax.rem(b, SLOTS)
        acc = None
        for t in range(tiles):
            d = jnp.dot(p_buf[:, t * TILE : (t + 1) * TILE], v_buf[slot, t * TILE : (t + 1) * TILE, :], preferred_element_type=jnp.float32)
            acc = d if acc is None else acc + d
        parts[me, b] = acc.astype(jnp.bfloat16)

    pltpu.make_async_copy(q_hbm, q_buf, q_sem).wait()
    k_copy(0).wait()
    stat = weigh(0, jnp.zeros((heads, LANES), jnp.float32))
    k_copy(SLOTS).start()

    def step(more_k, more_v, b, stat):
        k_copy(b + 1).wait()
        v_copy(b).wait()
        gather_values(b)
        stat = weigh(b + 1, stat)
        if more_v:
            v_copy(b + SLOTS).start()
        if more_k:
            k_copy(b + 1 + SLOTS).start()
        return stat

    def send(first, count, k):
        for peer in peers:
            to(peer, parts.at[me, first : first + count], send_sem.at[k], recv_sem.at[k]).start()

    begin = 0
    for end in (seqs // 4, seqs // 2, 3 * seqs // 4, seqs - 1 - SLOTS):
        stat = lax.fori_loop(begin, end, functools.partial(step, True, True), stat)
        if begin == 0:
            pl.semaphore_wait(barrier, n - 1)
        send(begin, end - begin, 0)
        begin = end
    stat = step(False, True, begin, stat)
    for b in range(begin + 1, seqs - 1):
        stat = step(False, False, b, stat)
    stats[me] = stat
    send(begin, seqs - 1 - begin, 0)
    for peer in peers:
        to(peer, stats.at[me], send_sem.at[1], recv_sem.at[1]).start()
    v_copy(seqs - 1).wait()
    gather_values(seqs - 1)
    send(seqs - 1, 1, 2)

    to(peers[0], stats.at[0 : n - 1], send_sem.at[1], recv_sem.at[1]).wait()
    seen = [stats[i] for i in range(n)]
    high = functools.reduce(jnp.maximum, seen)
    scale = [jnp.exp2((s - high) * log2e_scaled) for s in seen]
    total = sum(c * pltpu.roll(s, LANES // 2, 1) for c, s in zip(scale, seen))
    scale = [c / total for c in scale]

    def put(b):
        o_ref[b] = sum(scale[i][:, b : b + 1] * parts[i, b].astype(jnp.float32) for i in range(n)).astype(o_ref.dtype)

    to(peers[0], parts.at[0 : n - 1, 0 : seqs - 1], send_sem.at[0], recv_sem.at[0]).wait()
    for b in range(seqs - 1):
        put(b)
    to(peers[0], parts.at[0 : n - 1, 0], send_sem.at[2], recv_sem.at[2]).wait()
    put(seqs - 1)


def solution(mesh):
    n = mesh.shape["sp"]

    def step(q, k, v):
        seqs, tokens, heads, head = k.shape
        rows = tokens * heads
        return pl.pallas_call(
            functools.partial(kernel, n),
            out_shape=pltpu.VMEM(q.shape, q.dtype),
            in_specs=[pl.BlockSpec(memory_space=pl.ANY)] * 3,
            out_specs=pl.BlockSpec(memory_space=pltpu.VMEM),
            scratch_shapes=[
                pltpu.VMEM(q.shape, q.dtype),
                pltpu.VMEM((SLOTS, rows, head), k.dtype),
                pltpu.VMEM((SLOTS, rows, head), v.dtype),
                pltpu.VMEM((heads, rows), jnp.bfloat16),
                pltpu.VMEM((n, seqs, heads, head), jnp.bfloat16),
                pltpu.VMEM((n, heads, LANES), jnp.float32),
                pltpu.SemaphoreType.DMA,
                pltpu.SemaphoreType.DMA((SLOTS,)),
                pltpu.SemaphoreType.DMA((SLOTS,)),
                pltpu.SemaphoreType.DMA((3,)),
                pltpu.SemaphoreType.DMA((3,)),
            ],
            compiler_params=pltpu.CompilerParams(collective_id=0, has_side_effects=True),
        )(q, k.reshape(seqs, rows, head), v.reshape(seqs, rows, head))

    return jax.shard_map(
        step,
        mesh=mesh,
        in_specs=(P("dp", None, None), P("dp", "sp", None, None), P("dp", "sp", None, None)),
        out_specs=P("dp", None, None),
        check_vma=False,
    )
```

profile of v0, /device:TPU:0, one launch (start us, length us, event | category | flops | bytes accessed | tf_op | source)
XLA Modules:
  0.0 48.7 jit_solution(6345180694128718275)
XLA Ops:
  0.0 48.1 %shard_map.37 = bf16[32,8,256]{2,1,0:T(8,128)(2,1)S(1)} custom-call(bf16[32,8,256]{2,1,0:T(8,128)(2,1)} %q_hbm.1, bf16[32,4096,256]{2,1,0:T(8,128)(2,1)} %bitcast.k_hbm, bf16[32,4096,256]{2,1,0:T(8,128)(2,1)} %bitcast.1.v_hbm), custom_call_target="tpu_custom_call" | custom-call | tf_op jit(solution)/shard_map/pallas_call | solution.py:145
  48.1 0.7 %copy.5 = bf16[32,8,256]{2,1,0:T(8,128)(2,1)} copy(bf16[32,8,256]{2,1,0:T(8,128)(2,1)S(1)} %shard_map.37) | data formatting | bytes 262144
where the time goes:
time: 48.8 us; the launch traced here: 48.7 us
  Pallas kernels  48.1 us (99%)
  local copies, waits for them, and re-layouts  0.66 us (1%)
    pallas_call x1, Pallas kernels, step(): pl.pallas_call(functools.partial(kernel, n), out_shape=pltpu.VMEM(q.shape...  48.1 us

commit v1 on v0

v1 whole, which is shorter than its diff:
```python
import functools
import math

import jax
import jax.numpy as jnp
from jax import lax
from jax.experimental import pallas as pl
from jax.experimental.pallas import tpu as pltpu
from jax.sharding import PartitionSpec as P

K_SLOTS, V_SLOTS = 5, 7
FLIGHT = 5
LEAD = 3
PIECES = 1
TILE = 256
LANES = 128


def peers_of(me):
    x, y, core = me // 4, (me // 2) % 2, me % 2
    for dx, dy, dc in ((1, 1, 0), (1, 1, 1), (1, 0, 0), (1, 0, 1), (0, 1, 0), (0, 1, 1), (0, 0, 1)):
        px = 1 - x if dx else x
        py = 1 - y if dy else y
        pc = 1 - core if dc else core
        yield px * 4 + py * 2 + pc


def kernel(n, q_hbm, k_hbm, v_hbm, o_ref, q_buf, k_buf, v_buf, s_buf, p_buf, sums, parts, stats, q_sem, k_sem, v_sem, piece_sem, send_sem, recv_sem):
    seqs, rows, head = k_hbm.shape
    heads = q_hbm.shape[1]
    tiles = rows // TILE
    log2e_scaled = math.log2(math.e) * head**-0.5
    me = lax.axis_index("sp")
    peers = list(peers_of(me))

    def k_copy(b):
        slot = lax.rem(b, K_SLOTS)
        return pltpu.make_async_copy(k_hbm.at[b], k_buf.at[slot], k_sem.at[slot])

    def v_copy(b):
        slot = lax.rem(b, V_SLOTS)
        return pltpu.make_async_copy(v_hbm.at[b], v_buf.at[slot], v_sem.at[slot])

    def piece_copy(i):
        part = pl.ds(i * (rows // PIECES), rows // PIECES)
        return pltpu.make_async_copy(v_hbm.at[seqs - 1, part], v_buf.at[(seqs - 1) % V_SLOTS, part], piece_sem.at[i])

    queue = [(k_copy, b) for b in range(LEAD + 1)]
    for b in range(seqs - LEAD - 1):
        queue += [(v_copy, b), (k_copy, b + LEAD + 1)]
    queue += [(v_copy, b) for b in range(seqs - LEAD - 1, seqs - 1)] + [(piece_copy, i) for i in range(PIECES)]
    last = len(queue) - PIECES

    def start(first):
        for copy, b in queue[first : first + 1] if first < last else queue[last:] if first == last else ():
            copy(b).start()

    def to(peer, ref, send, recv):
        return pltpu.make_async_remote_copy(
            src_ref=ref, dst_ref=ref, send_sem=send, recv_sem=recv, device_id={"sp": peer}, device_id_type=pl.DeviceIdType.MESH
        )

    pltpu.make_async_copy(q_hbm, q_buf, q_sem).start()
    for i in range(FLIGHT):
        start(i)

    barrier = pltpu.get_barrier_semaphore()
    for peer in peers:
        pl.semaphore_signal(barrier, inc=1, device_id={"sp": peer}, device_id_type=pl.DeviceIdType.MESH)

    own = lax.broadcasted_iota(jnp.int32, (heads, TILE), 1) % heads == lax.broadcasted_iota(jnp.int32, (heads, TILE), 0)
    lane = lax.broadcasted_iota(jnp.int32, (heads, LANES), 1)

    def score(b):
        slot = lax.rem(b, K_SLOTS)
        q = q_buf[b]
        for t in range(tiles):
            s = lax.dot_general(q, k_buf[slot, t * TILE : (t + 1) * TILE, :], (((1,), (1,)), ((), ())), preferred_element_type=jnp.float32)
            s_buf[:, t * TILE : (t + 1) * TILE] = jnp.where(own, s, -jnp.inf)

    def weigh(b, stat):
        p_slot = lax.rem(b, LEAD - 1)
        scores = [s_buf[:, t * TILE : (t + 1) * TILE] for t in range(tiles)]
        high = jnp.max(functools.reduce(jnp.maximum, scores), -1, keepdims=True)
        total = None
        for t in range(tiles):
            w = jnp.exp2((scores[t] - high) * log2e_scaled)
            p_buf[p_slot, :, t * TILE : (t + 1) * TILE] = w.astype(jnp.bfloat16)
            total = w if total is None else total + w
        total = jnp.sum(total, -1, keepdims=True)
        return jnp.where(lane == b, high, jnp.where(lane == b + LANES // 2, total, stat))

    def gather_values(b, sums, first, count):
        slot, p_slot = lax.rem(b, V_SLOTS), lax.rem(b, LEAD - 1)
        sums = list(sums)
        for t in range(first, first + count):
            d = jnp.dot(p_buf[p_slot, :, t * TILE : (t + 1) * TILE], v_buf[slot, t * TILE : (t + 1) * TILE, :], preferred_element_type=jnp.float32)
            i = t % len(sums)
            sums[i] = d if sums[i] is None else sums[i] + d
        return sums

    def keep(b, sums):
        parts[me, b] = sum(sums[1:], sums[0]).astype(jnp.bfloat16)

    def halves(b, first, count, i):
        for h in range(2):
            (sums[i + h],) = gather_values(b, [None], first + h * (count // 2), count // 2)

    def finish(b, count):
        first = me // n
        keep(b, [sums[first + i] for i in range(count)])

    pltpu.make_async_copy(q_hbm, q_buf, q_sem).wait()
    stat = jnp.zeros((heads, LANES), jnp.float32)
    for b in range(LEAD):
        k_copy(b).wait()
        start(FLIGHT + b)
        if b >= 1:
            stat = weigh(b - 1, stat)
        score(b)

    def step(b, stat):
        k_copy(b + LEAD).wait()
        if isinstance(b, int):
            start(LEAD + 2 * b + FLIGHT)
        elif FLIGHT % 2:
            v_copy(b + FLIGHT // 2).start()
        else:
            k_copy(b + LEAD + FLIGHT // 2).start()
        v_copy(b).wait()
        if isinstance(b, int):
            start(LEAD + 2 * b + FLIGHT + 1)
        elif FLIGHT % 2:
            k_copy(b + LEAD + FLIGHT // 2 + 1).start()
        else:
            v_copy(b + FLIGHT // 2).start()
        keep(b, gather_values(b, [None], 0, tiles))
        stat = weigh(b + LEAD - 1, stat)
        score(b + LEAD)
        return stat

    def send(first, count, k):
        for peer in peers:
            to(peer, parts.at[me, first : first + count], send_sem.at[k], recv_sem.at[k]).start()

    begin = 0
    for end in (seqs // 4, seqs // 2, 3 * seqs // 4 - 2, (last - FLIGHT) // 2 - LEAD):
        stat = lax.fori_loop(begin, end, step, stat)
        if begin == 0:
            pl.semaphore_wait(barrier, n - 1)
        send(begin, end - begin, 0)
        begin = end
    for b in range(begin, seqs - LEAD):
        stat = step(b, stat)
        send(b, 1, 0)
    for b in range(seqs - LEAD, seqs - 1):
        v_copy(b).wait()
        halves(b, 0, tiles, 0)
        if b == seqs - LEAD:
            stat = weigh(seqs - 1, stat)
            stats[me] = stat
        finish(b, 2)
        send(b, 1, 0)
        if b == seqs - LEAD:
            for peer in peers:
                to(peer, stats.at[me], send_sem.at[1], recv_sem.at[1]).start()
    for i in range(PIECES):
        piece_copy(i).wait()
        halves(seqs - 1, i * (tiles // PIECES), tiles // PIECES, 2 * i)
    finish(seqs - 1, 2 * PIECES)
    send(seqs - 1, 1, 2)

    to(peers[0], stats.at[0 : n - 1], send_sem.at[1], recv_sem.at[1]).wait()
    seen = [stats[i] for i in range(n)]
    high = functools.reduce(jnp.maximum, seen)
    scale = [jnp.exp2((s - high) * log2e_scaled) for s in seen]
    total = sum(c * pltpu.roll(s, LANES // 2, 1) for c, s in zip(scale, seen))
    scale = [c / total for c in scale]

    def weights_of(b):
        return [jnp.broadcast_to(c[:, b : b + 1], (heads, head)) for c in scale]

    def put(b, weights):
        o_ref[b] = sum(w * parts[i, b].astype(jnp.float32) for i, w in enumerate(weights)).astype(o_ref.dtype)

    to(peers[0], parts.at[0 : n - 1, 0 : seqs - 1], send_sem.at[0], recv_sem.at[0]).wait()
    for b in range(seqs - 1):
        put(b, weights_of(b))
    weights = weights_of(seqs - 1)
    to(peers[0], parts.at[0 : n - 1, 0], send_sem.at[2], recv_sem.at[2]).wait()
    put(seqs - 1, weights)


def solution(mesh):
    n = mesh.shape["sp"]

    def step(q, k, v):
        seqs, tokens, heads, head = k.shape
        rows = tokens * heads
        return pl.pallas_call(
            functools.partial(kernel, n),
            out_shape=pltpu.VMEM(q.shape, q.dtype),
            in_specs=[pl.BlockSpec(memory_space=pl.ANY)] * 3,
            out_specs=pl.BlockSpec(memory_space=pltpu.VMEM),
            scratch_shapes=[
                pltpu.VMEM(q.shape, q.dtype),
                pltpu.VMEM((K_SLOTS, rows, head), k.dtype),
                pltpu.VMEM((V_SLOTS, rows, head), v.dtype),
                pltpu.VMEM((heads, rows), jnp.float32),
                pltpu.VMEM((LEAD - 1, heads, rows), jnp.bfloat16),
                pltpu.VMEM((2 * PIECES, heads, head), jnp.float32),
                pltpu.VMEM((n, seqs, heads, head), jnp.bfloat16),
                pltpu.VMEM((n, heads, LANES), jnp.float32),
                pltpu.SemaphoreType.DMA,
                pltpu.SemaphoreType.DMA((K_SLOTS,)),
                pltpu.SemaphoreType.DMA((V_SLOTS,)),
                pltpu.SemaphoreType.DMA((PIECES,)),
                pltpu.SemaphoreType.DMA((3,)),
                pltpu.SemaphoreType.DMA((3,)),
            ],
            compiler_params=pltpu.CompilerParams(collective_id=0, has_side_effects=True),
        )(q, k.reshape(seqs, rows, head), v.reshape(seqs, rows, head))

    return jax.shard_map(
        step,
        mesh=mesh,
        in_specs=(P("dp", None, None), P("dp", "sp", None, None), P("dp", "sp", None, None)),
        out_specs=P("dp", None, None),
        check_vma=False,
    )
```

time: 48.8 us -> 47 us (0.963)
  Pallas kernels: 48.1 us -> 46.2 us
    pallas_call x1, Pallas kernels: 48.1 us -> 46.2 us  [step(): pl.pallas_call(functools.partial(kernel, n), out_shape=pltpu.VMEM(q.shape...]
where the time goes in v1:
time: 47 us; the launch traced here: 46.9 us
  Pallas kernels  46.2 us (98%)
  local copies, waits for them, and re-layouts  0.66 us (1%)
    pallas_call x1, Pallas kernels, step(): pl.pallas_call(functools.partial(kernel, n), out_shape=pltpu.VMEM(q.shape...  46.2 us

profile of v1, /device:TPU:0, one launch (start us, length us, event | category | flops | bytes accessed | tf_op | source)
XLA Modules:
  0.0 46.9 jit_solution(5254439167922824038)
XLA Ops:
  0.0 46.2 %shard_map.37 = bf16[32,8,256]{2,1,0:T(8,128)(2,1)S(1)} custom-call(bf16[32,8,256]{2,1,0:T(8,128)(2,1)} %q_hbm.1, bf16[32,4096,256]{2,1,0:T(8,128)(2,1)} %bitcast.k_hbm, bf16[32,4096,256]{2,1,0:T(8,128)(2,1)} %bitcast.1.v_hbm), custom_call_target="tpu_custom_call" | custom-call | tf_op jit(solution)/shard_map/pallas_call | solution.py:200
  46.3 0.7 %copy.5 = bf16[32,8,256]{2,1,0:T(8,128)(2,1)} copy(bf16[32,8,256]{2,1,0:T(8,128)(2,1)S(1)} %shard_map.37) | data formatting | bytes 262144
